TPU v7x, 32 devices: a whole 2x2x4 slice. The times are simulated.
32 devices in a mesh: freq: 4 (over y, x), space: 8 (over z, core).
Axes of the slice: x: 2, y: 2, z: 4, core: 2. Of those that a mesh axis runs over, the one named last changes fastest.
Arguments:
- spectra: bfloat16 [64, 24576, 256], P('freq', 'space'), may hold values from -48 to 48, as said below
- weight: float32 [24576], P('space'), may hold values from 0.25 to 4
- partner: int32 [64], P('freq'), may hold values from 0 to 15
- counts: int32 [64], P('freq'), may hold values from 1 to 8
Outputs:
- modes: bfloat16 [64, 16, 24576], P('freq', None, 'space')
- energy: float32 [64, 8], P('freq')
- coherence: float32 [64, 2, 8, 8], P('freq')
Inputs may be any that keep to these rules, and one draw needn't show every extreme that they name: spectra are finite Fourier coefficients.
All inputs are finite; a program needn't handle non-finite values.
Results may differ from a plain program's by a relative error of at most 0.0045.
Values may be sent and summed in bfloat16 or wider, within the bound.
A program may use at most 128 MiB of HBM per device.

v0:
```python
import functools

import jax
import jax.numpy as jnp
from jax import lax
from jax.experimental import pallas as pl
from jax.experimental.pallas import tpu as pltpu
from jax.sharding import PartitionSpec as P

KMAX = 8
ITERS = 4
AHEAD = 4
LINK = jnp.bfloat16
MESH = pl.DeviceIdType.MESH
F32 = jnp.float32
BF16 = jnp.bfloat16


def dot(left, right, dims, precision=None):
    return lax.dot_general(
        left, right, (dims, ((), ())), precision=precision, preferred_element_type=F32
    )


def split(value):
    high = value.astype(BF16)
    return high, (value - high.astype(F32)).astype(BF16)


def pack(moments, half):
    real = moments[:half, :half] + moments[half:, half:]
    imag = moments[:half, half:] - moments[half:, :half]
    row = lax.broadcasted_iota(jnp.int32, (half, half), 0)
    col = lax.broadcasted_iota(jnp.int32, (half, half), 1)
    return jnp.where(row <= col, real, imag)


def unpack(packed, half):
    row = lax.broadcasted_iota(jnp.int32, (half, half), 0)
    col = lax.broadcasted_iota(jnp.int32, (half, half), 1)
    other = packed.T
    real = jnp.where(row <= col, packed, other)
    imag = jnp.where(row > col, packed, jnp.where(row < col, -other, 0.0))
    return real, imag


def orthonormal(real, imag):
    row = lax.broadcasted_iota(jnp.int32, real.shape, 0)
    for k in range(KMAX):
        a_re = jnp.broadcast_to(real[k : k + 1, :], real.shape)
        a_im = jnp.broadcast_to(imag[k : k + 1, :], imag.shape)
        norm = jnp.sum(a_re * a_re + a_im * a_im, axis=1, keepdims=True)
        p_re = jnp.sum(a_re * real + a_im * imag, axis=1, keepdims=True)
        p_im = jnp.sum(a_re * imag - a_im * real, axis=1, keepdims=True)
        inverse = 1.0 / jnp.sqrt(norm + 1e-06)
        e_re, e_im = a_re * inverse, a_im * inverse
        q_re, q_im = p_re * inverse, p_im * inverse
        later_re = real - q_re * e_re + q_im * e_im
        later_im = imag - q_re * e_im - q_im * e_re
        real = jnp.where(row > k, later_re, jnp.where(row == k, e_re, real))
        imag = jnp.where(row > k, later_im, jnp.where(row == k, e_im, imag))
    return real, imag


def apply_operator(operator, real, imag, half):
    high, low = split(jnp.concatenate([real, imag], axis=0))
    left = jnp.concatenate([high, high, low], axis=1)
    image = dot(left, operator, ((1,), (0,)))
    new_re = image[:KMAX, :half] + image[KMAX:, half:]
    new_im = image[KMAX:, :half] - image[:KMAX, half:]
    return new_re, new_im


def choose(cross, partner, groups):
    wide = 2 * KMAX * groups
    row = lax.broadcasted_iota(jnp.int32, (wide, wide), 0)
    col = lax.broadcasted_iota(jnp.int32, (wide, wide), 1)
    lane_group = col // (2 * KMAX)
    want = jnp.broadcast_to(partner[:, None, :], (groups, 2 * KMAX, partner.shape[1]))
    want = want.reshape(wide, partner.shape[1])
    kept = jnp.where(lane_group == want, cross, 0.0).reshape(groups, 2, KMAX, wide)
    top = kept[:, 0].reshape(groups * KMAX, wide)
    bottom = kept[:, 1].reshape(groups * KMAX, wide)
    from_place = row % (2 * KMAX)
    to_place = col % (2 * KMAX)
    same = jnp.where(from_place == to_place, 1.0, 0.0)
    swap = jnp.where(
        from_place == to_place + KMAX, 1.0, jnp.where(from_place == to_place - KMAX, -1.0, 0.0)
    )
    highest = lax.Precision.HIGHEST
    folded = dot(top, same, ((1,), (0,)), highest) + dot(bottom, swap, ((1,), (0,)), highest)
    shape = (groups * KMAX, wide)
    row_group = lax.broadcasted_iota(jnp.int32, shape, 0) // KMAX
    column_group = lax.broadcasted_iota(jnp.int32, shape, 1) // (2 * KMAX)
    folded = jnp.where(row_group == column_group, folded, 0.0)
    return jnp.sum(folded.reshape(groups, KMAX, wide), axis=0)


def kernel(
    n_freq, n_space, spectra, weight, partner, counts,
    modes_out, energy_out, coherence_out,
    held, columns, send, recv, message, modes, mirrored, scaled,
    partners, partials, arrived,
    load_sem, store_sem, gram_send, gram_recv, basis_send, basis_recv,
    modes_send, modes_recv, partner_send, partner_recv, part_send, part_recv,
):
    groups, points, width = held.shape
    half = width // 2
    part = points // 2
    own = groups // n_space
    total = points * n_space
    band = lax.axis_index("freq")
    me = lax.axis_index("space")
    opposite = n_freq - 1 - band
    upper = jnp.where(band > opposite, 1, 0)
    mine = pl.multiple_of(upper * part, 128)
    theirs = pl.multiple_of((1 - upper) * part, 128)

    def order(step):
        return lax.rem((me + 1) * own + step, groups)

    def load(step):
        f = order(step)
        return pltpu.make_async_copy(spectra.at[f], held.at[f], load_sem.at[f])

    for step in range(AHEAD):
        load(step).start()

    barrier = pltpu.get_barrier_semaphore()
    for apart in range(1, n_space):
        peer = lax.rem(me + apart, n_space)
        pl.semaphore_signal(barrier, inc=1, device_id=(band, peer), device_id_type=MESH)
    for apart in range(n_space):
        peer = lax.rem(me + apart, n_space)
        pl.semaphore_signal(barrier, inc=1, device_id=(opposite, peer), device_id_type=MESH)

    lane_row = lax.broadcasted_iota(jnp.int32, (groups, 128), 0)
    table = jnp.zeros((groups, 128), jnp.int32)
    for f in range(groups):
        table = jnp.where(lane_row == f, partner[f], table)
    partners[0] = table
    for block in range(points // 128):
        span = pl.ds(block * 128, 128)
        columns[span, :] = jnp.broadcast_to(weight[:, span], (128, 128)).T

    pl.semaphore_wait(barrier, 2 * n_space - 1)

    partner_copy = pltpu.make_async_remote_copy(
        src_ref=partners.at[0], dst_ref=partners.at[1], send_sem=partner_send,
        recv_sem=partner_recv, device_id=(opposite, me), device_id_type=MESH,
    )
    partner_copy.start()

    def gram_copy(f, source):
        owner = f // own
        slot = lax.rem(f, own)
        return pltpu.make_async_remote_copy(
            src_ref=send.at[f], dst_ref=recv.at[source, slot], send_sem=gram_send.at[f],
            recv_sem=gram_recv.at[source, slot], device_id=(band, owner), device_id_type=MESH,
        )

    def gram_step(step, carry):
        f = order(step)

        @pl.when(step + AHEAD < groups)
        def _():
            load(step + AHEAD).start()

        load(step).wait()
        block = held[f]
        scale = columns[...]
        weighted = (jnp.concatenate([scale, scale], axis=1) * block.astype(F32)).astype(BF16)
        packed = pack(dot(block, weighted, ((0,), (0,))), half).astype(LINK)
        owner = f // own

        @pl.when(owner != me)
        def _():
            send[f] = packed
            gram_copy(f, me).start()

        @pl.when(owner == me)
        def _():
            recv[me, lax.rem(f, own)] = packed

        return carry

    lax.fori_loop(0, groups, gram_step, 0)

    for apart in range(1, n_space):
        source = lax.rem(me + apart, n_space)
        for slot in range(own):
            gram_copy(source * own + slot, source).wait_send()
            pltpu.make_async_remote_copy(
                src_ref=send.at[0], dst_ref=recv.at[source, slot], send_sem=gram_send.at[0],
                recv_sem=gram_recv.at[source, slot], device_id=(band, source), device_id_type=MESH,
            ).wait_recv()

    operators, state = [], []
    for slot in range(own):
        packed = recv[0, slot].astype(F32)
        for source in range(1, n_space):
            packed = packed + recv[source, slot].astype(F32)
        real, imag = unpack(packed / total, half)
        high, low = split(jnp.concatenate([real, imag], axis=1))
        operators.append(jnp.concatenate([high, low, high], axis=0))
        state += [real[:KMAX], -imag[:KMAX]]

    def all_orthonormal(state):
        done = []
        for slot in range(own):
            done += orthonormal(state[2 * slot], state[2 * slot + 1])
        return tuple(done)

    def sweep(_, state):
        image = []
        for slot in range(own):
            image += apply_operator(operators[slot], state[2 * slot], state[2 * slot + 1], half)
        return all_orthonormal(image)

    state = lax.fori_loop(0, ITERS - 1, sweep, all_orthonormal(state))

    rank = lax.broadcasted_iota(jnp.int32, (KMAX, half), 0)
    for slot in range(own):
        f = me * own + slot
        real, imag = state[2 * slot], state[2 * slot + 1]
        image_re, image_im = apply_operator(operators[slot], real, imag, half)
        energy = jnp.sum(real * image_re + imag * image_im, axis=1, keepdims=True)
        energy = jnp.broadcast_to(energy, (KMAX, half))
        scale = jnp.where(rank < counts[f], 1.0 / jnp.sqrt(energy + 1e-06), 0.0)
        message[f] = jnp.concatenate([real * scale, imag * scale, energy], axis=0)

    def basis_copy(source, peer):
        span = pl.ds(source * own, own)
        return pltpu.make_async_remote_copy(
            src_ref=message.at[span], dst_ref=message.at[span], send_sem=basis_send.at[peer],
            recv_sem=basis_recv.at[source], device_id=(band, peer), device_id_type=MESH,
        )

    for apart in range(1, n_space):
        basis_copy(me, lax.rem(me + apart, n_space)).start()

    def modes_copy(f):
        return pltpu.make_async_remote_copy(
            src_ref=modes.at[f, :, pl.ds(theirs, part)], dst_ref=mirrored.at[f],
            send_sem=modes_send.at[f], recv_sem=modes_recv.at[f],
            device_id=(opposite, me), device_id_type=MESH,
        )

    def store(f):
        return pltpu.make_async_copy(modes.at[f], modes_out.at[f], store_sem.at[f])

    def modes_step(step, carry):
        f = lax.rem(me * own + step, groups)
        source = f // own

        @pl.when(jnp.logical_and(lax.rem(f, own) == 0, source != me))
        def _():
            basis_copy(source, source).wait_recv()

        basis = message[f]
        real, imag = basis[:KMAX], basis[KMAX : 2 * KMAX]
        coefficient = jnp.concatenate(
            [jnp.concatenate([real, -imag], axis=1), jnp.concatenate([imag, real], axis=1)], axis=0
        ).astype(BF16)
        modes[f] = dot(coefficient, held[f], ((1,), (1,))).astype(BF16)
        modes_copy(f).start()
        store(f).start()
        energy_out[f] = basis[2 * KMAX :]
        weighted = modes[f, :, pl.ds(mine, part)].astype(F32) * weight[:, pl.ds(mine, part)]
        high, low = split(weighted)
        scaled[0, f] = high
        scaled[1, f] = low
        return carry

    lax.fori_loop(0, groups, modes_step, 0)

    def modes_wait(f, carry):
        modes_copy(f).wait_recv()
        return carry

    partner_copy.wait()
    lax.fori_loop(0, groups, modes_wait, 0)
    wide = groups * 2 * KMAX
    psi = mirrored[...].reshape(wide, part)
    cross = dot(scaled[0].reshape(wide, part), psi, ((1,), (1,)))
    cross = (cross + dot(scaled[1].reshape(wide, part), psi, ((1,), (1,)))) / total
    spread = functools.partial(jnp.concatenate, axis=1)
    copies = wide // 128
    partials[0] = choose(cross, spread([partners[0]] * copies), groups)
    partials[1] = choose(cross.T, spread([partners[1]] * copies), groups)

    def part_copy(side, source, peer):
        across = opposite if side else band
        return pltpu.make_async_remote_copy(
            src_ref=partials.at[side], dst_ref=arrived.at[side, source],
            send_sem=part_send.at[side, peer], recv_sem=part_recv.at[side, source],
            device_id=(across, peer), device_id_type=MESH,
        )

    for apart in range(n_space):
        peer = lax.rem(me + apart, n_space)
        part_copy(1, me, peer).start()
        if apart:
            part_copy(0, me, peer).start()

    def drain(f, carry):
        modes_copy(f).wait_send()
        store(f).wait()
        return carry

    lax.fori_loop(0, groups, drain, 0)
    for apart in range(1, n_space):
        basis_copy(me, lax.rem(me + apart, n_space)).wait_send()

    result = partials[0]
    for apart in range(n_space):
        peer = lax.rem(me + apart, n_space)
        part_copy(1, peer, peer).wait()
        result = result + arrived[1, peer]
        if apart:
            part_copy(0, peer, peer).wait()
            result = result + arrived[0, peer]
    coherence_out[...] = result


def on_device(n_freq, n_space, spectra, weight, partner, counts):
    groups, points, width = spectra.shape
    half = width // 2
    own = groups // n_space
    rows = 2 * KMAX
    wide = groups * rows
    dma = pltpu.SemaphoreType.DMA
    vmem = pl.BlockSpec(memory_space=pltpu.VMEM)
    smem = pl.BlockSpec(memory_space=pltpu.SMEM)
    hbm = pl.BlockSpec(memory_space=pltpu.HBM)
    modes, energy, coherence = pl.pallas_call(
        functools.partial(kernel, n_freq, n_space),
        out_shape=(
            jax.ShapeDtypeStruct((groups, rows, points), BF16),
            jax.ShapeDtypeStruct((groups, KMAX, half), F32),
            jax.ShapeDtypeStruct((KMAX, wide), F32),
        ),
        in_specs=[hbm, vmem, smem, smem],
        out_specs=(hbm, vmem, vmem),
        scratch_shapes=[
            pltpu.VMEM((groups, points, width), BF16),
            pltpu.VMEM((points, 128), F32),
            pltpu.VMEM((groups, half, half), LINK),
            pltpu.VMEM((n_space, own, half, half), LINK),
            pltpu.VMEM((groups, 3 * KMAX, half), F32),
            pltpu.VMEM((groups, rows, points), BF16),
            pltpu.VMEM((groups, rows, points // 2), BF16),
            pltpu.VMEM((2, groups, rows, points // 2), BF16),
            pltpu.VMEM((2, groups, 128), jnp.int32),
            pltpu.VMEM((2, KMAX, wide), F32),
            pltpu.VMEM((2, n_space, KMAX, wide), F32),
            dma((groups,)),
            dma((groups,)),
            dma((groups,)),
            dma((n_space, own)),
            dma((n_space,)),
            dma((n_space,)),
            dma((groups,)),
            dma((groups,)),
            dma(()),
            dma(()),
            dma((2, n_space)),
            dma((2, n_space)),
        ],
        compiler_params=pltpu.CompilerParams(
            collective_id=0, has_side_effects=True, vmem_limit_bytes=60 * 1024 * 1024
        ),
    )(spectra, weight.reshape(1, points), partner, counts)
    coherence = coherence.reshape(KMAX, groups, 2, KMAX).transpose(1, 2, 0, 3)
    return modes, energy[:, :, 0], coherence


def solution(mesh):
    in_specs = (P("freq", "space", None), P("space"), P("freq"), P("freq"))
    out_specs = (P("freq", None, "space"), P("freq", None), P("freq", None, None, None))
    return jax.shard_map(
        functools.partial(on_device, mesh.shape["freq"], mesh.shape["space"]),
        mesh=mesh,
        in_specs=in_specs,
        out_specs=out_specs,
        check_vma=False,
    )
```

profile of v0, /device:TPU:0, one launch (start us, length us, event | category | flops | bytes accessed | tf_op | source)
XLA Modules:
  0.0 62.5 jit_solution(7100225365879574821)
XLA Ops:
  0.6 56.0 %shard_map.67 = (bf16[16,16,3072]{2,1,0:T(8,128)(2,1)}, f32[16,8,128]{2,1,0:T(8,128)}, f32[8,256]{1,0:T(8,128)}) custom-call(bf16[16,3072,256]{2,1,0:T(8,128)(2,1)} %spectra.1, f32[1,3072]{1,0:T(1,128)} %bitcast.6, s32[16]{0:T(128)} %partner.1, s32[16]{0:T(128)} %counts.1), custom_call_target="tpu_custom_call" | custom-call | tf_op jit(solution)/shard_map/pallas_call | solution.py:336
  56.6 1.5 %copy.9 = f32[16,8,1]{0,1,2:T(8,128)} copy(f32[16,8,1]{2,1,0:T(8,128)} %bitcast.5) | data formatting | bytes 1024 | tf_op jit(solution)/shard_map/slice | solution.py:375
  58.2 0.9 %reshape.13 = f32[8,16,2,8]{3,2,1,0:T(2,128)S(1)} reshape(f32[8,256]{1,0:T(8,128)} %get-tuple-element.8) | data formatting | bytes 16384 | tf_op jit(solution)/shard_map/reshape | solution.py:374
  59.1 0.7 %copy.10 = f32[16,2,8,8]{0,3,2,1:T(8,128)} copy(f32[16,2,8,8]{3,1,0,2:T(2,128)S(1)} %bitcast.4) | data formatting | bytes 16384
  59.9 2.7 %copy.12 = bf16[16,16,3072]{2,1,0:T(8,128)(2,1)} copy(bf16[16,16,3072]{2,1,0:T(8,128)(2,1)} %get-tuple-element.15) | data formatting | bytes 3145728
where the time goes:
time: 62.8 us; the launch traced here: 62.5 us
  Pallas kernels  56 us (89%)
  local copies, waits for them, and re-layouts  5.9 us (9%)
  between operations  0.65 us (1%)
    pallas_call x1, Pallas kernels, on_device(): pl.pallas_call(functools.partial(kernel, n_freq, n_space), out_shape=(jax...  56 us
    unnamed x2, local copies, waits for them, and re-layouts  3.43 us
    slice x1, local copies, waits for them, and re-layouts, on_device(): return (modes, energy[:, :, 0], coherence)  1.55 us

commit v1 on v0

v1 whole, which is shorter than its diff:
```python
import functools

import jax
import jax.numpy as jnp
from jax import lax
from jax.experimental import pallas as pl
from jax.experimental.pallas import tpu as pltpu
from jax.sharding import PartitionSpec as P

KMAX = 8
ROWS = 2 * KMAX
ITERS = 4
AHEAD = 4
EPS = 1e-06
LINK = jnp.bfloat16
MESH = pl.DeviceIdType.MESH
F32 = jnp.float32
BF16 = jnp.bfloat16


def dot(left, right, dims):
    return lax.dot_general(left, right, (dims, ((), ())), preferred_element_type=F32)


def split(value):
    high = value.astype(BF16)
    return high, (value - high.astype(F32)).astype(BF16)


def exclusive(left, right, size):
    result, bit = 0, 1
    while bit < size:
        result = result + bit * lax.rem(lax.div(left, bit) + lax.div(right, bit), 2)
        bit *= 2
    return result


def pack(moments, half):
    real = moments[:half, :half] + moments[half:, half:]
    imag = moments[:half, half:] - moments[half:, :half]
    row = lax.broadcasted_iota(jnp.int32, (half, half), 0)
    col = lax.broadcasted_iota(jnp.int32, (half, half), 1)
    return jnp.where(row <= col, real, imag)


def unpack(packed, half):
    row = lax.broadcasted_iota(jnp.int32, (half, half), 0)
    col = lax.broadcasted_iota(jnp.int32, (half, half), 1)
    other = packed.T
    real = jnp.where(row <= col, packed, other)
    imag = jnp.where(row > col, packed, jnp.where(row < col, -other, 0.0))
    return real, imag


def orthonormal(real, imag):
    shape = real.shape
    row = lax.broadcasted_iota(jnp.int32, shape, 0)

    def spread(value, k):
        return jnp.broadcast_to(value[k : k + 1, :], shape)

    table = []
    for k in range(KMAX):
        a_re, a_im = spread(real, k), spread(imag, k)
        s_re = jnp.sum(a_re * real + a_im * imag, axis=1, keepdims=True)
        s_im = jnp.sum(a_re * imag - a_im * real, axis=1, keepdims=True)
        table.append((jnp.broadcast_to(s_re, shape), jnp.broadcast_to(s_im, shape)))
    for k in range(KMAX):
        s_re, s_im = table[k]
        inverse = lax.rsqrt(jnp.maximum(spread(s_re, k), 0.0) + EPS)
        square = inverse * inverse
        a_re, a_im = spread(real, k), spread(imag, k)
        c_re, c_im = s_re * square, s_im * square
        later_re = real - c_re * a_re + c_im * a_im
        later_im = imag - c_re * a_im - c_im * a_re
        real = jnp.where(row > k, later_re, jnp.where(row == k, real * inverse, real))
        imag = jnp.where(row > k, later_im, jnp.where(row == k, imag * inverse, imag))
        factor = 1.0 + EPS * square
        d_re, d_im = c_re * factor, c_im * factor
        for m in range(k + 1, KMAX):
            m_re, m_im = spread(d_re, m), spread(d_im, m)
            t_re, t_im = table[m]
            table[m] = (
                t_re - (m_re * s_re + m_im * s_im),
                t_im - (m_re * s_im - m_im * s_re),
            )
    return real, imag


def apply_operator(operator, real, imag, half):
    high, low = split(jnp.concatenate([real, imag], axis=0))
    left = jnp.concatenate([high, high, low], axis=1)
    image = dot(left, operator, ((1,), (0,)))
    new_re = image[:KMAX, :half] + image[KMAX:, half:]
    new_im = image[KMAX:, :half] - image[:KMAX, half:]
    return new_re, new_im


def select(crosses, side, partner, groups):
    per = 128 // ROWS
    lane = lax.broadcasted_iota(jnp.int32, (ROWS, 128), 1)
    place = lax.rem(lax.broadcasted_iota(jnp.int32, (KMAX, 128), 1), ROWS)
    parts = []
    for first in range(0, groups, per):
        kept = jnp.zeros((ROWS, 128), F32)
        for f in range(first, first + per):
            block = crosses[side, partner[side, f]]
            kept = jnp.where(lax.div(lane, ROWS) == f - first, block[:, first * ROWS : first * ROWS + 128], kept)
        top, bottom = kept[:KMAX], kept[KMAX:]
        real = top + pltpu.roll(bottom, 128 - KMAX, 1)
        imag = pltpu.roll(bottom, KMAX, 1) - top
        parts.append(jnp.where(place < KMAX, real, imag))
    return jnp.concatenate(parts, axis=1)


def kernel(
    n_freq, n_space, spectra, weight_in, partner_in, counts_in,
    modes, energy_out, coherence_out,
    held, columns, weight, send, recv, coefs, energies, mirrored, scaled,
    crosses, partner_there, partials, arrived, partner, counts,
    load_sem, small_sem, gram_send, gram_recv, basis_send, basis_recv, energy_send, energy_recv,
    modes_send, modes_recv, partner_send, partner_recv, part_send, part_recv,
):
    groups, points, width = held.shape
    half = width // 2
    part = points // 2
    own = groups // n_space
    total = points * n_space
    band = lax.axis_index("freq")
    me = lax.axis_index("space")
    opposite = n_freq - 1 - band
    upper = jnp.where(band > opposite, 1, 0)
    mine = pl.multiple_of(upper * part, 128)
    theirs = pl.multiple_of((1 - upper) * part, 128)

    def owner_of(step):
        return exclusive(me, n_space - 1 - lax.rem(step, n_space), n_space)

    def order(step):
        return lax.div(step, n_space) * n_space + owner_of(step)

    def load(step):
        f = order(step)
        return pltpu.make_async_copy(spectra.at[f], held.at[f], load_sem.at[f])

    weight_copy = pltpu.make_async_copy(weight_in, weight, small_sem.at[0])
    weight_copy.start()
    for step in range(min(AHEAD, groups)):
        load(step).start()

    barrier = pltpu.get_barrier_semaphore()
    for apart in range(1, n_space):
        peer = lax.rem(me + apart, n_space)
        pl.semaphore_signal(barrier, inc=1, device_id=(band, peer), device_id_type=MESH)
    for apart in range(n_space):
        peer = lax.rem(me + apart, n_space)
        pl.semaphore_signal(barrier, inc=1, device_id=(opposite, peer), device_id_type=MESH)

    mine_copy = pltpu.make_async_copy(partner_in, partner.at[pl.ds(0, 1)], small_sem.at[1])
    counts_copy = pltpu.make_async_copy(counts_in, counts, small_sem.at[2])
    mine_copy.start()
    counts_copy.start()
    weight_copy.wait()
    for block in range(points // 128):
        span = pl.ds(block * 128, 128)
        columns[span, :] = jnp.broadcast_to(weight[:, span], (128, 128)).T

    def moments_of(step):
        f = order(step)

        @pl.when(step + AHEAD < groups)
        def _():
            load(step + AHEAD).start()

        load(step).wait()
        block = held[f]
        scale = columns[...]
        weighted = (jnp.concatenate([scale, scale], axis=1) * block.astype(F32)).astype(BF16)
        return pack(dot(block, weighted, ((0,), (0,))), half).astype(LINK)

    def gram_copy(f, source, peer):
        return pltpu.make_async_remote_copy(
            src_ref=send.at[f], dst_ref=recv.at[lax.div(f, n_space), source], send_sem=gram_send.at[f],
            recv_sem=gram_recv.at[lax.div(f, n_space), source], device_id=(band, peer), device_id_type=MESH,
        )

    def gram_step(step, carry):
        f, owner = order(step), owner_of(step)
        packed = moments_of(step)

        @pl.when(owner != me)
        def _():
            send[f] = packed
            gram_copy(f, me, owner).start()

        @pl.when(owner == me)
        def _():
            recv[lax.div(f, n_space), me] = packed

        return carry

    first = order(0)
    send[first] = moments_of(0)
    pl.semaphore_wait(barrier, 2 * n_space - 1)
    gram_copy(first, me, owner_of(0)).start()
    partner_copy = pltpu.make_async_remote_copy(
        src_ref=partner_in, dst_ref=partner_there, send_sem=partner_send,
        recv_sem=partner_recv, device_id=(opposite, me), device_id_type=MESH,
    )
    partner_copy.start()
    mine_copy.wait()
    counts_copy.wait()

    ahead = n_space + n_space // 2 if own > 1 else n_space
    lax.fori_loop(1, ahead, gram_step, 0)

    def basis_copy(f, peer):
        return pltpu.make_async_remote_copy(
            src_ref=coefs.at[f], dst_ref=coefs.at[f], send_sem=basis_send.at[lax.div(f, n_space), peer],
            recv_sem=basis_recv.at[f], device_id=(band, peer), device_id_type=MESH,
        )

    def energy_copy(f, peer):
        return pltpu.make_async_remote_copy(
            src_ref=energies.at[f], dst_ref=energies.at[f], send_sem=energy_send.at[lax.div(f, n_space), peer],
            recv_sem=energy_recv.at[f], device_id=(band, peer), device_id_type=MESH,
        )

    def solve(slot):
        f = slot * n_space + me
        for apart in range(1, n_space):
            source = lax.rem(me + apart, n_space)
            gram_copy(f, source, source).wait_recv()
        packed = recv[slot, 0].astype(F32)
        for source in range(1, n_space):
            packed = packed + recv[slot, source].astype(F32)
        real, imag = unpack(packed / total, half)
        high, low = split(jnp.concatenate([real, imag], axis=1))
        operator = jnp.concatenate([high, low, high], axis=0)
        real, imag = orthonormal(real[:KMAX], -imag[:KMAX])
        for _ in range(ITERS - 1):
            real, imag = orthonormal(*apply_operator(operator, real, imag, half))
        image_re, image_im = apply_operator(operator, real, imag, half)
        energy = jnp.sum(real * image_re + imag * image_im, axis=1, keepdims=True)
        energy = jnp.broadcast_to(energy, (KMAX, half))
        rank = lax.broadcasted_iota(jnp.int32, (KMAX, half), 0)
        scale = jnp.where(rank < counts[0, f], 1.0 / jnp.sqrt(energy + EPS), 0.0)
        coefs[f] = jnp.concatenate([real * scale, imag * scale], axis=0).astype(BF16)
        energies[f] = energy
        for apart in range(1, n_space):
            basis_copy(f, exclusive(me, n_space - apart, n_space)).start()
        for apart in range(1, n_space):
            energy_copy(f, exclusive(me, n_space - apart, n_space)).start()

    def modes_copy(f):
        return pltpu.make_async_remote_copy(
            src_ref=modes.at[f, :, pl.ds(theirs, part)], dst_ref=mirrored.at[f],
            send_sem=modes_send.at[f], recv_sem=modes_recv.at[f],
            device_id=(opposite, me), device_id_type=MESH,
        )

    def modes_step(slot, step):
        source = exclusive(me, step, n_space)
        f = slot * n_space + source

        @pl.when(step > 0)
        def _():
            basis_copy(f, source).wait_recv()

        basis = coefs[f].astype(F32)
        real, imag = basis[:KMAX], basis[KMAX:]
        coefficient = jnp.concatenate(
            [jnp.concatenate([real, -imag], axis=1), jnp.concatenate([imag, real], axis=1)], axis=0
        ).astype(BF16)
        modes[f] = dot(coefficient, held[f], ((1,), (1,))).astype(BF16)
        modes_copy(f).start()
        weighted = modes[f, :, pl.ds(mine, part)].astype(F32) * weight[:, pl.ds(mine, part)]
        high, low = split(weighted)
        scaled[0, f] = high
        scaled[1, f] = low

    for slot in range(own):
        solve(slot)
        rest = groups - ahead if slot == 0 else 0

        def both(step, carry, slot=slot):
            modes_step(slot, step)
            return gram_step(ahead + step, carry)

        def alone(step, carry, slot=slot):
            modes_step(slot, step)
            return carry

        mixed = min(rest, n_space)
        if mixed:
            lax.fori_loop(0, mixed, both, 0)
        if rest > mixed:
            lax.fori_loop(ahead + mixed, groups, gram_step, 0)
        if mixed < n_space:
            lax.fori_loop(mixed, n_space, alone, 0)

    partner_copy.wait()
    there_copy = pltpu.make_async_copy(partner_there, partner.at[pl.ds(1, 1)], small_sem.at[1])
    there_copy.start()

    lane = lax.broadcasted_iota(jnp.int32, (KMAX, half), 1)
    gathered = jnp.zeros((KMAX, half), F32)
    for f in range(groups):
        slot, source = f // n_space, f % n_space

        @pl.when(source != me)
        def _(f=f, source=source):
            energy_copy(f, source).wait_recv()

        gathered = jnp.where(lane == f, energies[f], gathered)
    energy_out[...] = gathered
    there_copy.wait()

    def modes_wait(f, carry):
        modes_copy(f).wait_recv()
        return carry

    lax.fori_loop(0, groups, modes_wait, 0)
    wide = groups * ROWS
    psi = mirrored[...].reshape(wide, part)
    cross = dot(scaled[0].reshape(wide, part), psi, ((1,), (1,)))
    cross = (cross + dot(scaled[1].reshape(wide, part), psi, ((1,), (1,)))) / total
    crosses[0] = cross.T.reshape(groups, ROWS, wide)
    crosses[1] = cross.reshape(groups, ROWS, wide)
    partials[1] = select(crosses, 1, partner, groups)
    partials[0] = select(crosses, 0, partner, groups)

    def part_copy(side, source, peer):
        across = opposite if side else band
        return pltpu.make_async_remote_copy(
            src_ref=partials.at[side], dst_ref=arrived.at[side, source],
            send_sem=part_send.at[side, peer], recv_sem=part_recv.at[side, source],
            device_id=(across, peer), device_id_type=MESH,
        )

    for apart in range(n_space - 1, -1, -1):
        peer = exclusive(me, apart, n_space)
        part_copy(1, me, peer).start()
        if apart:
            part_copy(0, me, peer).start()

    def drain(f, carry):
        modes_copy(f).wait_send()
        return carry

    lax.fori_loop(0, groups, drain, 0)
    for step in range(groups):
        f = order(step)
        if step % n_space != n_space - 1:
            gram_copy(f, me, me).wait_send()
    for slot in range(own):
        for apart in range(1, n_space):
            peer = exclusive(me, apart, n_space)
            basis_copy(slot * n_space + me, peer).wait_send()
            energy_copy(slot * n_space + me, peer).wait_send()

    result = partials[0]
    for apart in range(n_space):
        peer = exclusive(me, apart, n_space)
        part_copy(1, peer, peer).wait()
        result = result + arrived[1, peer]
        if apart:
            part_copy(0, peer, peer).wait()
            result = result + arrived[0, peer]
    coherence_out[...] = result


def finish(modes, energy, coherence, modes_out, energy_out, coherence_out, few, blocks, sems):
    groups = energy_out.shape[1]
    wide = groups * ROWS
    modes_copy = pltpu.make_async_copy(modes, modes_out, sems.at[2])
    modes_copy.start()
    few[...] = energy[:, :groups]
    energy_copy = pltpu.make_async_copy(few, energy_out, sems.at[0])
    energy_copy.start()
    value = coherence[...]
    high, low = split(value)
    lowest = (value - high.astype(F32) - low.astype(F32)).astype(BF16)
    row = lax.broadcasted_iota(jnp.int32, (wide, wide), 0)
    col = lax.broadcasted_iota(jnp.int32, (wide, wide), 1)
    source = lax.rem(col, groups) * ROWS + lax.div(col, groups)
    move = jnp.where(row == source, 1.0, 0.0).astype(BF16)
    moved = dot(high, move, ((1,), (0,))) + dot(low, move, ((1,), (0,))) + dot(lowest, move, ((1,), (0,)))
    for place in range(ROWS):
        blocks[place] = moved[:, place * groups : (place + 1) * groups]
    coherence_copy = pltpu.make_async_copy(blocks, coherence_out, sems.at[1])
    coherence_copy.start()
    energy_copy.wait()
    coherence_copy.wait()
    modes_copy.wait()


def on_device(n_freq, n_space, spectra, weight, partner, counts):
    groups, points, width = spectra.shape
    half = width // 2
    own = groups // n_space
    wide = groups * ROWS
    dma = pltpu.SemaphoreType.DMA
    vmem = pl.BlockSpec(memory_space=pltpu.VMEM)
    hbm = pl.BlockSpec(memory_space=pltpu.HBM)
    modes, energy, coherence = pl.pallas_call(
        functools.partial(kernel, n_freq, n_space),
        out_shape=(
            pltpu.VMEM((groups, ROWS, points), BF16),
            pltpu.VMEM((KMAX, half), F32),
            pltpu.VMEM((KMAX, wide), F32),
        ),
        in_specs=[hbm, hbm, hbm, hbm],
        out_specs=(vmem, vmem, vmem),
        scratch_shapes=[
            pltpu.VMEM((groups, points, width), BF16),
            pltpu.VMEM((points, 128), F32),
            pltpu.VMEM((1, points), F32),
            pltpu.VMEM((groups, half, half), LINK),
            pltpu.VMEM((own, n_space, half, half), LINK),
            pltpu.VMEM((groups, ROWS, half), BF16),
            pltpu.VMEM((groups, KMAX, half), F32),
            pltpu.VMEM((groups, ROWS, points // 2), BF16),
            pltpu.VMEM((2, groups, ROWS, points // 2), BF16),
            pltpu.VMEM((2, groups, ROWS, wide), F32),
            pltpu.VMEM((1, groups), jnp.int32),
            pltpu.VMEM((2, KMAX, wide), F32),
            pltpu.VMEM((2, n_space, KMAX, wide), F32),
            pltpu.SMEM((2, groups), jnp.int32),
            pltpu.SMEM((1, groups), jnp.int32),
            dma((groups,)),
            dma((3,)),
            dma((groups,)),
            dma((own, n_space)),
            dma((own, n_space)),
            dma((groups,)),
            dma((own, n_space)),
            dma((groups,)),
            dma((groups,)),
            dma((groups,)),
            dma(()),
            dma(()),
            dma((2, n_space)),
            dma((2, n_space)),
        ],
        compiler_params=pltpu.CompilerParams(
            collective_id=0, has_side_effects=True, vmem_limit_bytes=60 * 1024 * 1024
        ),
    )(spectra, weight.reshape(1, points), partner.reshape(1, groups), counts.reshape(1, groups))
    modes = pltpu.with_memory_space_constraint(modes, pltpu.VMEM)
    energy = pltpu.with_memory_space_constraint(energy, pltpu.VMEM)
    coherence = pltpu.with_memory_space_constraint(coherence, pltpu.VMEM)
    modes, energy, coherence = pl.pallas_call(
        finish,
        out_shape=(
            jax.ShapeDtypeStruct((groups, ROWS, points), BF16),
            jax.ShapeDtypeStruct((KMAX, groups), F32),
            jax.ShapeDtypeStruct((ROWS, KMAX, groups), F32),
        ),
        in_specs=[vmem, vmem, vmem],
        out_specs=(hbm, hbm, hbm),
        scratch_shapes=[
            pltpu.VMEM((KMAX, groups), F32),
            pltpu.VMEM((ROWS, KMAX, groups), F32),
            dma((3,)),
        ],
    )(modes, energy, coherence)
    coherence = coherence.reshape(2, KMAX, KMAX, groups).transpose(3, 0, 1, 2)
    return modes, energy.T, coherence


def solution(mesh):
    in_specs = (P("freq", "space", None), P("space"), P("freq"), P("freq"))
    out_specs = (P("freq", None, "space"), P("freq", None), P("freq", None, None, None))
    return jax.shard_map(
        functools.partial(on_device, mesh.shape["freq"], mesh.shape["space"]),
        mesh=mesh,
        in_specs=in_specs,
        out_specs=out_specs,
        check_vma=False,
    )
```

time: 62.8 us -> 50.4 us (0.80)
  Pallas kernels: 56 us -> 49.6 us
  local copies, waits for them, and re-layouts: 5.9 us -> 0 us
    pallas_call x1 -> x2, Pallas kernels: 56 us -> 49.6 us  [the longest x1 48.4 us: on_device(): pl.pallas_call(functools.partial(kernel, n_freq, n_space), out_shape=(plt...]
    unnamed x2 -> x0, local copies, waits for them, and re-layouts: 3.43 us -> none
    slice x1 -> x0, local copies, waits for them, and re-layouts: 1.55 us -> none  [on_device(): return (modes, energy[:, :, 0], coherence)]
    reshape x1 -> x0, local copies, waits for them, and re-layouts: 0.92 us -> none  [on_device(): coherence = coherence.reshape(KMAX, groups, 2, KMAX).transpose(1, 2, 0, 3)]
where the time goes in v1:
time: 50.4 us; the launch traced here: 50.2 us
  Pallas kernels  49.6 us (98%)
  between operations  0.64 us (1%)
    pallas_call x1, Pallas kernels, on_device(): pl.pallas_call(functools.partial(kernel, n_freq, n_space), out_shape=(plt...  48.4 us
    pallas_call x1, Pallas kernels, on_device(): pl.pallas_call(finish, out_shape=(jax.ShapeDtypeStruct((groups, ROWS, poi...  1.18 us

profile of v1, /device:TPU:0, one launch (start us, length us, event | category | flops | bytes accessed | tf_op | source)
XLA Modules:
  0.0 50.2 jit_solution(14846583184516782260)
XLA Ops:
  0.6 48.4 %shard_map.67 = (bf16[16,16,3072]{2,1,0:T(8,128)(2,1)S(1)}, f32[8,128]{1,0:T(8,128)S(1)}, f32[8,256]{1,0:T(8,128)S(1)}) custom-call(bf16[16,3072,256]{2,1,0:T(8,128)(2,1)} %spectra.1, f32[1,3072]{1,0:T(1,128)} %bitcast.7, s32[1,16]{1,0:T(1,128)} %bitcast.8, s32[1,16]{1,0:T(1,128)} %bitcast.9), custom_call_target="tpu_custom_call" | custom-call | tf_op jit(solution)/shard_map/pallas_call | solution.py:406
  49.0 1.2 %shard_map.68 = (bf16[16,16,3072]{2,1,0:T(8,128)(2,1)}, f32[8,16]{1,0:T(8,128)}, f32[16,8,16]{2,1,0:T(8,128)}) custom-call(bf16[16,16,3072]{2,1,0:T(8,128)(2,1)S(1)} %get-tuple-element.9.modes, f32[8,128]{1,0:T(8,128)S(1)} %get-tuple-element.10.energy, f32[8,256]{1,0:T(8,128)S(1)} %get-tuple-element.11.coherence), custom_call_target="tpu_custom_call" | custom-call | tf_op jit(solution)/shard_map/pallas_call | solution.py:453

commit v2 on v1

--- a/solution.py
+++ b/solution.py
@@ -116,36 +116,37 @@
 def kernel(
     n_freq, n_space, spectra, weight_in, partner_in, counts_in,
     modes, energy_out, coherence_out,
-    held, columns, weight, send, recv, coefs, energies, mirrored, scaled,
+    ring, held, weight, relay, relayed, kept, send, recv, mine_sum, coefs, energies, mirrored, scaled,
     crosses, partner_there, partials, arrived, partner, counts,
-    load_sem, small_sem, gram_send, gram_recv, basis_send, basis_recv, energy_send, energy_recv,
-    modes_send, modes_recv, partner_send, partner_recv, part_send, part_recv,
+    load_sem, small_sem, relay_send, relay_recv, gram_send, gram_recv, basis_send, basis_recv,
+    energy_send, energy_recv, modes_send, modes_recv, partner_send, partner_recv, part_send, part_recv,
 ):
-    groups, points, width = held.shape
+    groups, width, points = held.shape
     half = width // 2
     part = points // 2
     own = groups // n_space
+    chips = n_space // 2
+    wide = groups * ROWS
     total = points * n_space
     band = lax.axis_index("freq")
     me = lax.axis_index("space")
     opposite = n_freq - 1 - band
+    beside = exclusive(me, 1, n_space)
     upper = jnp.where(band > opposite, 1, 0)
     mine = pl.multiple_of(upper * part, 128)
     theirs = pl.multiple_of((1 - upper) * part, 128)
 
-    def owner_of(step):
-        return exclusive(me, n_space - 1 - lax.rem(step, n_space), n_space)
-
     def order(step):
-        return lax.div(step, n_space) * n_space + owner_of(step)
+        owner = exclusive(me, n_space - 1 - lax.rem(step, n_space), n_space)
+        return lax.div(step, n_space) * n_space + owner
 
     def load(step):
-        f = order(step)
-        return pltpu.make_async_copy(spectra.at[f], held.at[f], load_sem.at[f])
+        place = lax.rem(step, AHEAD)
+        return pltpu.make_async_copy(spectra.at[order(step)], ring.at[place], load_sem.at[place])
 
     weight_copy = pltpu.make_async_copy(weight_in, weight, small_sem.at[0])
     weight_copy.start()
-    for step in range(min(AHEAD, groups)):
+    for step in range(AHEAD):
         load(step).start()
 
     barrier = pltpu.get_barrier_semaphore()
@@ -161,48 +162,61 @@
     mine_copy.start()
     counts_copy.start()
     weight_copy.wait()
-    for block in range(points // 128):
-        span = pl.ds(block * 128, 128)
-        columns[span, :] = jnp.broadcast_to(weight[:, span], (128, 128)).T
-
-    def moments_of(step):
-        f = order(step)
-
-        @pl.when(step + AHEAD < groups)
+
+    def gram_pair(pair):
+        packed = []
+        for step in (2 * pair, 2 * pair + 1):
+            load(step).wait()
+        for step in (2 * pair, 2 * pair + 1):
+            block = ring[lax.rem(step, AHEAD)]
+            flipped = block.T
+            held[order(step)] = flipped
+            weighted = (flipped.astype(F32) * weight[...]).astype(BF16)
+            packed.append(pack(dot(weighted, block, ((1,), (0,))), half))
+        relay[pair] = packed[0]
+        kept[pair] = packed[1]
+
+        @pl.when(2 * pair + AHEAD < groups)
         def _():
-            load(step + AHEAD).start()
-
-        load(step).wait()
-        block = held[f]
-        scale = columns[...]
-        weighted = (jnp.concatenate([scale, scale], axis=1) * block.astype(F32)).astype(BF16)
-        return pack(dot(block, weighted, ((0,), (0,))), half).astype(LINK)
-
-    def gram_copy(f, source, peer):
+            load(2 * pair + AHEAD).start()
+            load(2 * pair + 1 + AHEAD).start()
+
+    def relay_copy(pair):
         return pltpu.make_async_remote_copy(
-            src_ref=send.at[f], dst_ref=recv.at[lax.div(f, n_space), source], send_sem=gram_send.at[f],
-            recv_sem=gram_recv.at[lax.div(f, n_space), source], device_id=(band, peer), device_id_type=MESH,
+            src_ref=relay.at[pair], dst_ref=relayed.at[pair], send_sem=relay_send,
+            recv_sem=relay_recv.at[pair], device_id=(band, beside), device_id_type=MESH,
         )
 
-    def gram_step(step, carry):
-        f, owner = order(step), owner_of(step)
-        packed = moments_of(step)
-
-        @pl.when(owner != me)
+    def gram_copy(slot, place):
+        peer = exclusive(me, n_space - 2 - 2 * place, n_space)
+        return pltpu.make_async_remote_copy(
+            src_ref=send.at[slot, place], dst_ref=recv.at[slot, place], send_sem=gram_send,
+            recv_sem=gram_recv.at[slot], device_id=(band, peer), device_id_type=MESH,
+        )
+
+    def forward(pair):
+        slot, place = lax.div(pair, chips), lax.rem(pair, chips)
+        relay_copy(pair).wait_recv()
+        chip = kept[pair] + relayed[pair]
+
+        @pl.when(place < chips - 1)
         def _():
-            send[f] = packed
-            gram_copy(f, me, owner).start()
-
-        @pl.when(owner == me)
+            send[slot, place] = chip.astype(LINK)
+            gram_copy(slot, place).start()
+
+        @pl.when(place == chips - 1)
         def _():
-            recv[lax.div(f, n_space), me] = packed
-
+            mine_sum[slot] = chip
+
+    def gram_step(pair, carry):
+        gram_pair(pair)
+        relay_copy(pair).start()
+        forward(pair - 1)
         return carry
 
-    first = order(0)
-    send[first] = moments_of(0)
+    gram_pair(0)
     pl.semaphore_wait(barrier, 2 * n_space - 1)
-    gram_copy(first, me, owner_of(0)).start()
+    relay_copy(0).start()
     partner_copy = pltpu.make_async_remote_copy(
         src_ref=partner_in, dst_ref=partner_there, send_sem=partner_send,
         recv_sem=partner_recv, device_id=(opposite, me), device_id_type=MESH,
@@ -211,29 +225,33 @@
     mine_copy.wait()
     counts_copy.wait()
 
-    ahead = n_space + n_space // 2 if own > 1 else n_space
-    lax.fori_loop(1, ahead, gram_step, 0)
+    pairs = own * chips
+    rest = chips // 2 if own > 1 else 0
+    lax.fori_loop(1, pairs - rest, gram_step, 0)
+    if not rest:
+        forward(pairs - 1)
 
     def basis_copy(f, peer):
         return pltpu.make_async_remote_copy(
-            src_ref=coefs.at[f], dst_ref=coefs.at[f], send_sem=basis_send.at[lax.div(f, n_space), peer],
+            src_ref=coefs.at[f], dst_ref=coefs.at[f], send_sem=basis_send,
             recv_sem=basis_recv.at[f], device_id=(band, peer), device_id_type=MESH,
         )
 
-    def energy_copy(f, peer):
+    def energy_copy(span, peer):
         return pltpu.make_async_remote_copy(
-            src_ref=energies.at[f], dst_ref=energies.at[f], send_sem=energy_send.at[lax.div(f, n_space), peer],
-            recv_sem=energy_recv.at[f], device_id=(band, peer), device_id_type=MESH,
+            src_ref=energies.at[span], dst_ref=energies.at[span], send_sem=energy_send,
+            recv_sem=energy_recv, device_id=(band, peer), device_id_type=MESH,
         )
 
     def solve(slot):
         f = slot * n_space + me
-        for apart in range(1, n_space):
-            source = lax.rem(me + apart, n_space)
-            gram_copy(f, source, source).wait_recv()
-        packed = recv[slot, 0].astype(F32)
-        for source in range(1, n_space):
-            packed = packed + recv[slot, source].astype(F32)
+        pltpu.make_async_remote_copy(
+            src_ref=send.at[slot], dst_ref=recv.at[slot], send_sem=gram_send,
+            recv_sem=gram_recv.at[slot], device_id=(band, beside), device_id_type=MESH,
+        ).wait_recv()
+        packed = mine_sum[slot]
+        for place in range(chips - 1):
+            packed = packed + recv[slot, place].astype(F32)
         real, imag = unpack(packed / total, half)
         high, low = split(jnp.concatenate([real, imag], axis=1))
         operator = jnp.concatenate([high, low, high], axis=0)
@@ -250,12 +268,12 @@
         for apart in range(1, n_space):
             basis_copy(f, exclusive(me, n_space - apart, n_space)).start()
         for apart in range(1, n_space):
-            energy_copy(f, exclusive(me, n_space - apart, n_space)).start()
+            energy_copy(pl.ds(f, 1), exclusive(me, n_space - apart, n_space)).start()
 
     def modes_copy(f):
         return pltpu.make_async_remote_copy(
             src_ref=modes.at[f, :, pl.ds(theirs, part)], dst_ref=mirrored.at[f],
-            send_sem=modes_send.at[f], recv_sem=modes_recv.at[f],
+            send_sem=modes_send, recv_sem=modes_recv.at[lax.div(f, n_space)],
             device_id=(opposite, me), device_id_type=MESH,
         )
 
@@ -272,7 +290,7 @@
         coefficient = jnp.concatenate(
             [jnp.concatenate([real, -imag], axis=1), jnp.concatenate([imag, real], axis=1)], axis=0
         ).astype(BF16)
-        modes[f] = dot(coefficient, held[f], ((1,), (1,))).astype(BF16)
+        modes[f] = dot(coefficient, held[f], ((1,), (0,))).astype(BF16)
         modes_copy(f).start()
         weighted = modes[f, :, pl.ds(mine, part)].astype(F32) * weight[:, pl.ds(mine, part)]
         high, low = split(weighted)
@@ -281,92 +299,89 @@
 
     for slot in range(own):
         solve(slot)
-        rest = groups - ahead if slot == 0 else 0
-
-        def both(step, carry, slot=slot):
-            modes_step(slot, step)
-            return gram_step(ahead + step, carry)
 
         def alone(step, carry, slot=slot):
             modes_step(slot, step)
             return carry
 
-        mixed = min(rest, n_space)
-        if mixed:
-            lax.fori_loop(0, mixed, both, 0)
-        if rest > mixed:
-            lax.fori_loop(ahead + mixed, groups, gram_step, 0)
-        if mixed < n_space:
-            lax.fori_loop(mixed, n_space, alone, 0)
+        if slot == 0 and rest:
+
+            def both(turn, carry):
+                lax.fori_loop(2 * turn, 2 * turn + 2, alone, 0)
+                return gram_step(pairs - rest + turn, carry)
+
+            lax.fori_loop(0, rest, both, 0)
+            lax.fori_loop(2 * rest, 2 * rest + 2, alone, 0)
+            forward(pairs - 1)
+            lax.fori_loop(2 * rest + 2, n_space, alone, 0)
+        else:
+            lax.fori_loop(0, n_space, alone, 0)
 
     partner_copy.wait()
     there_copy = pltpu.make_async_copy(partner_there, partner.at[pl.ds(1, 1)], small_sem.at[1])
     there_copy.start()
-
+    sent = pl.ds(0, own * (n_space - 1))
+    energy_copy(sent, beside).wait()
     lane = lax.broadcasted_iota(jnp.int32, (KMAX, half), 1)
     gathered = jnp.zeros((KMAX, half), F32)
     for f in range(groups):
-        slot, source = f // n_space, f % n_space
-
-        @pl.when(source != me)
-        def _(f=f, source=source):
-            energy_copy(f, source).wait_recv()
-
         gathered = jnp.where(lane == f, energies[f], gathered)
     energy_out[...] = gathered
+    pltpu.make_async_remote_copy(
+        src_ref=coefs.at[sent], dst_ref=coefs.at[sent], send_sem=basis_send,
+        recv_sem=basis_recv.at[0], device_id=(band, beside), device_id_type=MESH,
+    ).wait_send()
+    pltpu.make_async_remote_copy(
+        src_ref=relay, dst_ref=relayed, send_sem=relay_send,
+        recv_sem=relay_recv.at[0], device_id=(band, beside), device_id_type=MESH,
+    ).wait_send()
+    pltpu.make_async_remote_copy(
+        src_ref=send, dst_ref=recv, send_sem=gram_send,
+        recv_sem=gram_recv.at[0], device_id=(band, beside), device_id_type=MESH,
+    ).wait_send()
     there_copy.wait()
 
-    def modes_wait(f, carry):
-        modes_copy(f).wait_recv()
-        return carry
-
-    lax.fori_loop(0, groups, modes_wait, 0)
-    wide = groups * ROWS
-    psi = mirrored[...].reshape(wide, part)
-    cross = dot(scaled[0].reshape(wide, part), psi, ((1,), (1,)))
-    cross = (cross + dot(scaled[1].reshape(wide, part), psi, ((1,), (1,)))) / total
-    crosses[0] = cross.T.reshape(groups, ROWS, wide)
-    crosses[1] = cross.reshape(groups, ROWS, wide)
+    for slot in range(own):
+        span = pl.ds(slot * n_space, n_space)
+        pltpu.make_async_remote_copy(
+            src_ref=mirrored.at[span], dst_ref=mirrored.at[span], send_sem=modes_send,
+            recv_sem=modes_recv.at[slot], device_id=(opposite, me), device_id_type=MESH,
+        ).wait_recv()
+        rows = n_space * ROWS
+        psi = mirrored[span].reshape(rows, part)
+        cross = dot(psi, scaled[0].reshape(wide, part), ((1,), (1,)))
+        cross = (cross + dot(psi, scaled[1].reshape(wide, part), ((1,), (1,)))) / total
+        crosses[0, span] = cross.reshape(n_space, ROWS, wide)
+        crosses[1, :, :, slot * rows : (slot + 1) * rows] = cross.T.reshape(groups, ROWS, rows)
     partials[1] = select(crosses, 1, partner, groups)
     partials[0] = select(crosses, 0, partner, groups)
 
-    def part_copy(side, source, peer):
+    def part_copy(side, peer):
         across = opposite if side else band
         return pltpu.make_async_remote_copy(
-            src_ref=partials.at[side], dst_ref=arrived.at[side, source],
-            send_sem=part_send.at[side, peer], recv_sem=part_recv.at[side, source],
-            device_id=(across, peer), device_id_type=MESH,
+            src_ref=partials.at[side], dst_ref=arrived.at[side * n_space + me],
+            send_sem=part_send, recv_sem=part_recv, device_id=(across, peer), device_id_type=MESH,
         )
 
     for apart in range(n_space - 1, -1, -1):
         peer = exclusive(me, apart, n_space)
-        part_copy(1, me, peer).start()
+        part_copy(1, peer).start()
         if apart:
-            part_copy(0, me, peer).start()
-
-    def drain(f, carry):
-        modes_copy(f).wait_send()
-        return carry
-
-    lax.fori_loop(0, groups, drain, 0)
-    for step in range(groups):
-        f = order(step)
-        if step % n_space != n_space - 1:
-            gram_copy(f, me, me).wait_send()
-    for slot in range(own):
-        for apart in range(1, n_space):
-            peer = exclusive(me, apart, n_space)
-            basis_copy(slot * n_space + me, peer).wait_send()
-            energy_copy(slot * n_space + me, peer).wait_send()
-
-    result = partials[0]
-    for apart in range(n_space):
-        peer = exclusive(me, apart, n_space)
-        part_copy(1, peer, peer).wait()
-        result = result + arrived[1, peer]
-        if apart:
-            part_copy(0, peer, peer).wait()
-            result = result + arrived[0, peer]
+            part_copy(0, peer).start()
+
+    arrived[me] = partials[0]
+    pltpu.make_async_remote_copy(
+        src_ref=mirrored, dst_ref=mirrored, send_sem=modes_send,
+        recv_sem=modes_recv.at[0], device_id=(opposite, me), device_id_type=MESH,
+    ).wait_send()
+    there = pl.ds(0, 2 * n_space - 1)
+    pltpu.make_async_remote_copy(
+        src_ref=arrived.at[there], dst_ref=arrived.at[there], send_sem=part_send,
+        recv_sem=part_recv, device_id=(band, beside), device_id_type=MESH,
+    ).wait()
+    result = arrived[0]
+    for place in range(1, 2 * n_space):
+        result = result + arrived[place]
     coherence_out[...] = result
 
 
@@ -413,11 +428,15 @@
         in_specs=[hbm, hbm, hbm, hbm],
         out_specs=(vmem, vmem, vmem),
         scratch_shapes=[
-            pltpu.VMEM((groups, points, width), BF16),
-            pltpu.VMEM((points, 128), F32),
+            pltpu.VMEM((AHEAD, points, width), BF16),
+            pltpu.VMEM((groups, width, points), BF16),
             pltpu.VMEM((1, points), F32),
-            pltpu.VMEM((groups, half, half), LINK),
-            pltpu.VMEM((own, n_space, half, half), LINK),
+            pltpu.VMEM((groups // 2, half, half), F32),
+            pltpu.VMEM((groups // 2, half, half), F32),
+            pltpu.VMEM((groups // 2, half, half), F32),
+            pltpu.VMEM((own, n_space // 2 - 1, half, half), LINK),
+            pltpu.VMEM((own, n_space // 2 - 1, half, half), LINK),
+            pltpu.VMEM((own, half, half), F32),
             pltpu.VMEM((groups, ROWS, half), BF16),
             pltpu.VMEM((groups, KMAX, half), F32),
             pltpu.VMEM((groups, ROWS, points // 2), BF16),
@@ -425,23 +444,25 @@
             pltpu.VMEM((2, groups, ROWS, wide), F32),
             pltpu.VMEM((1, groups), jnp.int32),
             pltpu.VMEM((2, KMAX, wide), F32),
-            pltpu.VMEM((2, n_space, KMAX, wide), F32),
+            pltpu.VMEM((2 * n_space, KMAX, wide), F32),
             pltpu.SMEM((2, groups), jnp.int32),
             pltpu.SMEM((1, groups), jnp.int32),
+            dma((AHEAD,)),
+            dma((3,)),
+            dma(()),
+            dma((groups // 2,)),
+            dma(()),
+            dma((own,)),
+            dma(()),
             dma((groups,)),
-            dma((3,)),
-            dma((groups,)),
-            dma((own, n_space)),
-            dma((own, n_space)),
-            dma((groups,)),
-            dma((own, n_space)),
-            dma((groups,)),
-            dma((groups,)),
-            dma((groups,)),
-            dma(()),
-            dma(()),
-            dma((2, n_space)),
-            dma((2, n_space)),
+            dma(()),
+            dma(()),
+            dma(()),
+            dma((own,)),
+            dma(()),
+            dma(()),
+            dma(()),
+            dma(()),
         ],
         compiler_params=pltpu.CompilerParams(
             collective_id=0, has_side_effects=True, vmem_limit_bytes=60 * 1024 * 1024

time: 50.4 us -> 44.5 us (0.88)
  Pallas kernels: 49.6 us -> 43.7 us
    pallas_call x1, Pallas kernels: 48.4 us -> 42.5 us  [on_device(): pl.pallas_call(functools.partial(kernel, n_freq, n_space), out_shape=(plt...]
where the time goes in v2:
time: 44.5 us; the launch traced here: 44.3 us
  Pallas kernels  43.7 us (98%)
  between operations  0.64 us (1%)
    pallas_call x1, Pallas kernels, on_device(): pl.pallas_call(functools.partial(kernel, n_freq, n_space), out_shape=(plt...  42.5 us
    pallas_call x1, Pallas kernels, on_device(): pl.pallas_call(finish, out_shape=(jax.ShapeDtypeStruct((groups, ROWS, poi...  1.18 us

profile of v2, /device:TPU:0, one launch (start us, length us, event | category | flops | bytes accessed | tf_op | source)
XLA Modules:
  0.0 44.3 jit_solution(7747028171742643941)
XLA Ops:
  0.6 42.5 %shard_map.67 = (bf16[16,16,3072]{2,1,0:T(8,128)(2,1)S(1)}, f32[8,128]{1,0:T(8,128)S(1)}, f32[8,256]{1,0:T(8,128)S(1)}) custom-call(bf16[16,3072,256]{2,1,0:T(8,128)(2,1)} %spectra.1, f32[1,3072]{1,0:T(1,128)} %bitcast.7, s32[1,16]{1,0:T(1,128)} %bitcast.8, s32[1,16]{1,0:T(1,128)} %bitcast.9), custom_call_target="tpu_custom_call" | custom-call | tf_op jit(solution)/shard_map/pallas_call | solution.py:421
  43.2 1.2 %shard_map.68 = (bf16[16,16,3072]{2,1,0:T(8,128)(2,1)}, f32[8,16]{1,0:T(8,128)}, f32[16,8,16]{2,1,0:T(8,128)}) custom-call(bf16[16,16,3072]{2,1,0:T(8,128)(2,1)S(1)} %get-tuple-element.9.modes, f32[8,128]{1,0:T(8,128)S(1)} %get-tuple-element.10.energy, f32[8,256]{1,0:T(8,128)S(1)} %get-tuple-element.11.coherence), custom_call_target="tpu_custom_call" | custom-call | tf_op jit(solution)/shard_map/pallas_call | solution.py:474

commit v3 on v2

--- a/solution.py
+++ b/solution.py
@@ -10,7 +10,7 @@
 KMAX = 8
 ROWS = 2 * KMAX
 ITERS = 4
-AHEAD = 4
+AHEAD = 6
 EPS = 1e-06
 LINK = jnp.bfloat16
 MESH = pl.DeviceIdType.MESH
@@ -146,7 +146,7 @@
 
     weight_copy = pltpu.make_async_copy(weight_in, weight, small_sem.at[0])
     weight_copy.start()
-    for step in range(AHEAD):
+    for step in range(2):
         load(step).start()
 
     barrier = pltpu.get_barrier_semaphore()
@@ -162,11 +162,19 @@
     mine_copy.start()
     counts_copy.start()
     weight_copy.wait()
+    for step in range(2, 4):
+        load(step).start()
 
     def gram_pair(pair):
         packed = []
         for step in (2 * pair, 2 * pair + 1):
             load(step).wait()
+
+        @pl.when(2 * pair + 4 < groups)
+        def _():
+            load(2 * pair + 4).start()
+            load(2 * pair + 5).start()
+
         for step in (2 * pair, 2 * pair + 1):
             block = ring[lax.rem(step, AHEAD)]
             flipped = block.T
@@ -175,11 +183,6 @@
             packed.append(pack(dot(weighted, block, ((1,), (0,))), half))
         relay[pair] = packed[0]
         kept[pair] = packed[1]
-
-        @pl.when(2 * pair + AHEAD < groups)
-        def _():
-            load(2 * pair + AHEAD).start()
-            load(2 * pair + 1 + AHEAD).start()
 
     def relay_copy(pair):
         return pltpu.make_async_remote_copy(
@@ -293,9 +296,7 @@
         modes[f] = dot(coefficient, held[f], ((1,), (0,))).astype(BF16)
         modes_copy(f).start()
         weighted = modes[f, :, pl.ds(mine, part)].astype(F32) * weight[:, pl.ds(mine, part)]
-        high, low = split(weighted)
-        scaled[0, f] = high
-        scaled[1, f] = low
+        scaled[f] = weighted.astype(BF16)
 
     for slot in range(own):
         solve(slot)
@@ -349,12 +350,12 @@
         ).wait_recv()
         rows = n_space * ROWS
         psi = mirrored[span].reshape(rows, part)
-        cross = dot(psi, scaled[0].reshape(wide, part), ((1,), (1,)))
-        cross = (cross + dot(psi, scaled[1].reshape(wide, part), ((1,), (1,)))) / total
-        crosses[0, span] = cross.reshape(n_space, ROWS, wide)
-        crosses[1, :, :, slot * rows : (slot + 1) * rows] = cross.T.reshape(groups, ROWS, rows)
-    partials[1] = select(crosses, 1, partner, groups)
-    partials[0] = select(crosses, 0, partner, groups)
+        cross = dot(scaled[...].reshape(wide, part), psi, ((1,), (1,))) / total
+        crosses[0, span] = cross.T.reshape(n_space, ROWS, wide)
+        crosses[1, :, :, slot * rows : (slot + 1) * rows] = cross.reshape(groups, ROWS, rows)
+    partials[1] = select(crosses, 1, partner, groups).astype(LINK)
+    partial = select(crosses, 0, partner, groups)
+    partials[0] = partial.astype(LINK)
 
     def part_copy(side, peer):
         across = opposite if side else band
@@ -369,7 +370,7 @@
         if apart:
             part_copy(0, peer).start()
 
-    arrived[me] = partials[0]
+    arrived[me] = jnp.zeros(arrived.shape[1:], LINK)
     pltpu.make_async_remote_copy(
         src_ref=mirrored, dst_ref=mirrored, send_sem=modes_send,
         recv_sem=modes_recv.at[0], device_id=(opposite, me), device_id_type=MESH,
@@ -379,9 +380,9 @@
         src_ref=arrived.at[there], dst_ref=arrived.at[there], send_sem=part_send,
         recv_sem=part_recv, device_id=(band, beside), device_id_type=MESH,
     ).wait()
-    result = arrived[0]
-    for place in range(1, 2 * n_space):
-        result = result + arrived[place]
+    result = partial
+    for place in range(2 * n_space):
+        result = result + arrived[place].astype(F32)
     coherence_out[...] = result
 
 
@@ -440,11 +441,11 @@
             pltpu.VMEM((groups, ROWS, half), BF16),
             pltpu.VMEM((groups, KMAX, half), F32),
             pltpu.VMEM((groups, ROWS, points // 2), BF16),
-            pltpu.VMEM((2, groups, ROWS, points // 2), BF16),
+            pltpu.VMEM((groups, ROWS, points // 2), BF16),
             pltpu.VMEM((2, groups, ROWS, wide), F32),
             pltpu.VMEM((1, groups), jnp.int32),
-            pltpu.VMEM((2, KMAX, wide), F32),
-            pltpu.VMEM((2 * n_space, KMAX, wide), F32),
+            pltpu.VMEM((2, KMAX, wide), LINK),
+            pltpu.VMEM((2 * n_space, KMAX, wide), LINK),
             pltpu.SMEM((2, groups), jnp.int32),
             pltpu.SMEM((1, groups), jnp.int32),
             dma((AHEAD,)),

time: 44.5 us -> 43 us (0.966)
  Pallas kernels: 43.7 us -> 42.2 us
    pallas_call x1, Pallas kernels: 42.5 us -> 41 us  [on_device(): pl.pallas_call(functools.partial(kernel, n_freq, n_space), out_shape=(plt...]
where the time goes in v3:
time: 43 us; the launch traced here: 42.8 us
  Pallas kernels  42.2 us (98%)
  between operations  0.64 us (1%)
    pallas_call x1, Pallas kernels, on_device(): pl.pallas_call(functools.partial(kernel, n_freq, n_space), out_shape=(plt...  41 us
    pallas_call x1, Pallas kernels, on_device(): pl.pallas_call(finish, out_shape=(jax.ShapeDtypeStruct((groups, ROWS, poi...  1.18 us

profile of v3, /device:TPU:0, one launch (start us, length us, event | category | flops | bytes accessed | tf_op | source)
XLA Modules:
  0.0 42.8 jit_solution(10380532931932600097)
XLA Ops:
  0.6 41.0 %shard_map.67 = (bf16[16,16,3072]{2,1,0:T(8,128)(2,1)S(1)}, f32[8,128]{1,0:T(8,128)S(1)}, f32[8,256]{1,0:T(8,128)S(1)}) custom-call(bf16[16,3072,256]{2,1,0:T(8,128)(2,1)} %spectra.1, f32[1,3072]{1,0:T(1,128)} %bitcast.7, s32[1,16]{1,0:T(1,128)} %bitcast.8, s32[1,16]{1,0:T(1,128)} %bitcast.9), custom_call_target="tpu_custom_call" | custom-call | tf_op jit(solution)/shard_map/pallas_call | solution.py:422
  41.6 1.2 %shard_map.68 = (bf16[16,16,3072]{2,1,0:T(8,128)(2,1)}, f32[8,16]{1,0:T(8,128)}, f32[16,8,16]{2,1,0:T(8,128)}) custom-call(bf16[16,16,3072]{2,1,0:T(8,128)(2,1)S(1)} %get-tuple-element.9.modes, f32[8,128]{1,0:T(8,128)S(1)} %get-tuple-element.10.energy, f32[8,256]{1,0:T(8,128)S(1)} %get-tuple-element.11.coherence), custom_call_target="tpu_custom_call" | custom-call | tf_op jit(solution)/shard_map/pallas_call | solution.py:475

commit v4 on v3

--- a/solution.py
+++ b/solution.py
@@ -33,6 +33,14 @@
         result = result + bit * lax.rem(lax.div(left, bit) + lax.div(right, bit), 2)
         bit *= 2
     return result
+
+
+def when(condition, body):
+    if isinstance(condition, bool):
+        if condition:
+            body()
+    else:
+        pl.when(condition)(body)
 
 
 def pack(moments, half):
@@ -131,7 +139,8 @@
     band = lax.axis_index("freq")
     me = lax.axis_index("space")
     opposite = n_freq - 1 - band
-    beside = exclusive(me, 1, n_space)
+    peers = [exclusive(me, apart, n_space) for apart in range(n_space)]
+    beside = peers[1]
     upper = jnp.where(band > opposite, 1, 0)
     mine = pl.multiple_of(upper * part, 128)
     theirs = pl.multiple_of((1 - upper) * part, 128)
@@ -170,10 +179,11 @@
         for step in (2 * pair, 2 * pair + 1):
             load(step).wait()
 
-        @pl.when(2 * pair + 4 < groups)
-        def _():
+        def more():
             load(2 * pair + 4).start()
             load(2 * pair + 5).start()
+
+        when(2 * pair + 4 < groups, more)
 
         for step in (2 * pair, 2 * pair + 1):
             block = ring[lax.rem(step, AHEAD)]
@@ -198,18 +208,22 @@
         )
 
     def forward(pair):
-        slot, place = lax.div(pair, chips), lax.rem(pair, chips)
+        if isinstance(pair, int):
+            slot, place = pair // chips, pair % chips
+        else:
+            slot, place = lax.div(pair, chips), lax.rem(pair, chips)
         relay_copy(pair).wait_recv()
         chip = kept[pair] + relayed[pair]
 
-        @pl.when(place < chips - 1)
-        def _():
+        def away():
             send[slot, place] = chip.astype(LINK)
             gram_copy(slot, place).start()
 
-        @pl.when(place == chips - 1)
-        def _():
+        def here():
             mine_sum[slot] = chip
+
+        when(place < chips - 1, away)
+        when(place == chips - 1, here)
 
     def gram_step(pair, carry):
         gram_pair(pair)
@@ -230,7 +244,8 @@
 
     pairs = own * chips
     rest = chips // 2 if own > 1 else 0
-    lax.fori_loop(1, pairs - rest, gram_step, 0)
+    for pair in range(1, pairs - rest):
+        gram_step(pair, 0)
     if not rest:
         forward(pairs - 1)
 
@@ -268,10 +283,8 @@
         scale = jnp.where(rank < counts[0, f], 1.0 / jnp.sqrt(energy + EPS), 0.0)
         coefs[f] = jnp.concatenate([real * scale, imag * scale], axis=0).astype(BF16)
         energies[f] = energy
-        for apart in range(1, n_space):
-            basis_copy(f, exclusive(me, n_space - apart, n_space)).start()
-        for apart in range(1, n_space):
-            energy_copy(pl.ds(f, 1), exclusive(me, n_space - apart, n_space)).start()
+        for peer in reversed(peers[1:]):
+            basis_copy(f, peer).start()
 
     def modes_copy(f):
         return pltpu.make_async_remote_copy(
@@ -281,12 +294,10 @@
         )
 
     def modes_step(slot, step):
-        source = exclusive(me, step, n_space)
+        source = peers[step] if isinstance(step, int) else exclusive(me, step, n_space)
         f = slot * n_space + source
 
-        @pl.when(step > 0)
-        def _():
-            basis_copy(f, source).wait_recv()
+        when(step > 0, lambda: basis_copy(f, source).wait_recv())
 
         basis = coefs[f].astype(F32)
         real, imag = basis[:KMAX], basis[KMAX:]
@@ -300,6 +311,9 @@
 
     for slot in range(own):
         solve(slot)
+        modes_step(slot, 0)
+        for peer in reversed(peers[1:]):
+            energy_copy(pl.ds(slot * n_space + me, 1), peer).start()
 
         def alone(step, carry, slot=slot):
             modes_step(slot, step)
@@ -308,7 +322,7 @@
         if slot == 0 and rest:
 
             def both(turn, carry):
-                lax.fori_loop(2 * turn, 2 * turn + 2, alone, 0)
+                lax.fori_loop(jnp.maximum(2 * turn, 1), 2 * turn + 2, alone, 0)
                 return gram_step(pairs - rest + turn, carry)
 
             lax.fori_loop(0, rest, both, 0)
@@ -316,7 +330,7 @@
             forward(pairs - 1)
             lax.fori_loop(2 * rest + 2, n_space, alone, 0)
         else:
-            lax.fori_loop(0, n_space, alone, 0)
+            lax.fori_loop(1, n_space, alone, 0)
 
     partner_copy.wait()
     there_copy = pltpu.make_async_copy(partner_there, partner.at[pl.ds(1, 1)], small_sem.at[1])
@@ -365,10 +379,9 @@
         )
 
     for apart in range(n_space - 1, -1, -1):
-        peer = exclusive(me, apart, n_space)
-        part_copy(1, peer).start()
+        part_copy(1, peers[apart]).start()
         if apart:
-            part_copy(0, peer).start()
+            part_copy(0, peers[apart]).start()
 
     arrived[me] = jnp.zeros(arrived.shape[1:], LINK)
     pltpu.make_async_remote_copy(

time: 43 us -> 42.9 us (level)
  no operation moved by 1% of the time
where the time goes in v4:
time: 42.9 us; the launch traced here: 42.7 us
  Pallas kernels  42.1 us (98%)
  between operations  0.64 us (1%)
    pallas_call x1, Pallas kernels, on_device(): pl.pallas_call(functools.partial(kernel, n_freq, n_space), out_shape=(plt...  40.9 us
    pallas_call x1, Pallas kernels, on_device(): pl.pallas_call(finish, out_shape=(jax.ShapeDtypeStruct((groups, ROWS, poi...  1.18 us

profile of v4, /device:TPU:0, one launch (start us, length us, event | category | flops | bytes accessed | tf_op | source)
XLA Modules:
  0.0 42.7 jit_solution(13595724105911023311)
XLA Ops:
  0.6 40.9 %shard_map.67 = (bf16[16,16,3072]{2,1,0:T(8,128)(2,1)S(1)}, f32[8,128]{1,0:T(8,128)S(1)}, f32[8,256]{1,0:T(8,128)S(1)}) custom-call(bf16[16,3072,256]{2,1,0:T(8,128)(2,1)} %spectra.1, f32[1,3072]{1,0:T(1,128)} %bitcast.7, s32[1,16]{1,0:T(1,128)} %bitcast.8, s32[1,16]{1,0:T(1,128)} %bitcast.9), custom_call_target="tpu_custom_call" | custom-call | tf_op jit(solution)/shard_map/pallas_call | solution.py:435
  41.5 1.2 %shard_map.68 = (bf16[16,16,3072]{2,1,0:T(8,128)(2,1)}, f32[8,16]{1,0:T(8,128)}, f32[16,8,16]{2,1,0:T(8,128)}) custom-call(bf16[16,16,3072]{2,1,0:T(8,128)(2,1)S(1)} %get-tuple-element.9.modes, f32[8,128]{1,0:T(8,128)S(1)} %get-tuple-element.10.energy, f32[8,256]{1,0:T(8,128)S(1)} %get-tuple-element.11.coherence), custom_call_target="tpu_custom_call" | custom-call | tf_op jit(solution)/shard_map/pallas_call | solution.py:488

commit v5 on v4

--- a/solution.py
+++ b/solution.py
@@ -304,8 +304,15 @@
         coefficient = jnp.concatenate(
             [jnp.concatenate([real, -imag], axis=1), jnp.concatenate([imag, real], axis=1)], axis=0
         ).astype(BF16)
-        modes[f] = dot(coefficient, held[f], ((1,), (0,))).astype(BF16)
-        modes_copy(f).start()
+        if isinstance(step, int):
+            for first in (theirs, mine):
+                span = pl.ds(first, part)
+                modes[f, :, span] = dot(coefficient, held[f, :, span], ((1,), (0,))).astype(BF16)
+                if first is theirs:
+                    modes_copy(f).start()
+        else:
+            modes[f] = dot(coefficient, held[f], ((1,), (0,))).astype(BF16)
+            modes_copy(f).start()
         weighted = modes[f, :, pl.ds(mine, part)].astype(F32) * weight[:, pl.ds(mine, part)]
         scaled[f] = weighted.astype(BF16)
 
@@ -368,8 +375,6 @@
         crosses[0, span] = cross.T.reshape(n_space, ROWS, wide)
         crosses[1, :, :, slot * rows : (slot + 1) * rows] = cross.reshape(groups, ROWS, rows)
     partials[1] = select(crosses, 1, partner, groups).astype(LINK)
-    partial = select(crosses, 0, partner, groups)
-    partials[0] = partial.astype(LINK)
 
     def part_copy(side, peer):
         across = opposite if side else band
@@ -380,8 +385,10 @@
 
     for apart in range(n_space - 1, -1, -1):
         part_copy(1, peers[apart]).start()
-        if apart:
-            part_copy(0, peers[apart]).start()
+    partial = select(crosses, 0, partner, groups)
+    partials[0] = partial.astype(LINK)
+    for apart in range(n_space - 1, 0, -1):
+        part_copy(0, peers[apart]).start()
 
     arrived[me] = jnp.zeros(arrived.shape[1:], LINK)
     pltpu.make_async_remote_copy(

time: 42.9 us -> 42.9 us (level)
  no operation moved by 1% of the time
where the time goes in v5:
time: 42.9 us; the launch traced here: 42.7 us
  Pallas kernels  42 us (98%)
  between operations  0.64 us (1%)
    pallas_call x1, Pallas kernels, on_device(): pl.pallas_call(functools.partial(kernel, n_freq, n_space), out_shape=(plt...  40.9 us
    pallas_call x1, Pallas kernels, on_device(): pl.pallas_call(finish, out_shape=(jax.ShapeDtypeStruct((groups, ROWS, poi...  1.18 us

profile of v5, /device:TPU:0, one launch (start us, length us, event | category | flops | bytes accessed | tf_op | source)
XLA Modules:
  0.0 42.7 jit_solution(17835241260129920350)
XLA Ops:
  0.6 40.9 %shard_map.67 = (bf16[16,16,3072]{2,1,0:T(8,128)(2,1)S(1)}, f32[8,128]{1,0:T(8,128)S(1)}, f32[8,256]{1,0:T(8,128)S(1)}) custom-call(bf16[16,3072,256]{2,1,0:T(8,128)(2,1)} %spectra.1, f32[1,3072]{1,0:T(1,128)} %bitcast.7, s32[1,16]{1,0:T(1,128)} %bitcast.8, s32[1,16]{1,0:T(1,128)} %bitcast.9), custom_call_target="tpu_custom_call" | custom-call | tf_op jit(solution)/shard_map/pallas_call | solution.py:442
  41.5 1.2 %shard_map.68 = (bf16[16,16,3072]{2,1,0:T(8,128)(2,1)}, f32[8,16]{1,0:T(8,128)}, f32[16,8,16]{2,1,0:T(8,128)}) custom-call(bf16[16,16,3072]{2,1,0:T(8,128)(2,1)S(1)} %get-tuple-element.9.modes, f32[8,128]{1,0:T(8,128)S(1)} %get-tuple-element.10.energy, f32[8,256]{1,0:T(8,128)S(1)} %get-tuple-element.11.coherence), custom_call_target="tpu_custom_call" | custom-call | tf_op jit(solution)/shard_map/pallas_call | solution.py:495
